TPU v7x, 32 devices: a whole 2x2x4 slice. The times are simulated.
32 devices in a mesh: mem: 8 (over z, x), geo: 4 (over y, core).
Axes of the slice: x: 2, y: 2, z: 4, core: 2. Of those that a mesh axis runs over, the one named last changes fastest.
Arguments:
- control: float32 [8, 32, 48, 384], P('mem', 'geo'), may hold values from -6 to 6
- kappa_table: float32 [16], replicated, may hold values from 0.02 to 0.24
- kappa_index: int32 [48, 384], replicated, may hold values from 0 to 15
- tile_bounds: int32 [5], replicated, may hold values from 0 to 18432, as said below
- filter_bands: float32 [4, 5, 32], replicated, may hold values from -0.3 to 0.3
- perturbation: bfloat16 [2, 8, 32, 18432], P(None, 'mem', None, 'geo'), may hold values from -6 to 6
Outputs:
- increment: float32 [2, 32, 18432], P(None, 'mem', 'geo')
Inputs may be any that keep to these rules, and one draw needn't show every extreme that they name: tile_bounds[0] is 0, tile_bounds[4] is 18432, and the bounds never fall; tile t holds columns tile_bounds[t] to tile_bounds[t + 1] - 1.
All inputs are finite; a program needn't handle non-finite values.
Results may differ from a plain program's by a relative error of at most 0.005.
Values may be sent and summed in bfloat16 or wider, within the bound.
A program may use at most 64 MiB of HBM per device.

v0:
```python
import jax
import jax.numpy as jnp
from jax import lax
from jax.sharding import PartitionSpec as P

ITERS = 10


def neighbours(state):
    east = jnp.concatenate([state[..., 1:, :], state[..., -1:, :]], axis=-2)
    west = jnp.concatenate([state[..., :1, :], state[..., :-1, :]], axis=-2)
    north = jnp.concatenate([state[..., 1:], state[..., -1:]], axis=-1)
    south = jnp.concatenate([state[..., :1], state[..., :-1]], axis=-1)
    return (east, west, north, south)


def face_weights(kappa_field):
    return tuple((0.5 * (kappa_field + other) for other in neighbours(kappa_field)))


def diffuse_step(state, weights):
    east, west, north, south = neighbours(state)
    update = weights[0] * (east - state) + weights[1] * (west - state)
    update = update + weights[2] * (north - state) + weights[3] * (south - state)
    return state + update


def vertical_filter(values, coefficients):
    levels = values.shape[0]
    padded = jnp.pad(values, ((2, 2), (0, 0)))
    result = values
    for offset in range(5):
        result = result + coefficients[offset] * padded[offset : offset + levels]
    return result


def body(control, kappa_table, kappa_index, tile_bounds, filter_bands, perturbation):
    moved_pert = lax.all_to_all(perturbation, "mem", split_axis=2, concat_axis=1, tiled=True)
    kappa_field = jnp.zeros(kappa_index.shape, jnp.float32)
    for entry in range(kappa_table.shape[0]):
        kappa_field = kappa_field + jnp.where(kappa_index == entry, kappa_table[entry], 0.0)
    weights = face_weights(kappa_field)
    state_field = lax.fori_loop(0, ITERS, lambda step, cur: diffuse_step(cur, weights), control)
    flattened = state_field.reshape(state_field.shape[0], state_field.shape[1], -1)
    by_columns = lax.all_to_all(flattened, "geo", split_axis=2, concat_axis=1, tiled=True)
    width = by_columns.shape[2]
    tiles_count = filter_bands.shape[0]
    columns = lax.axis_index("geo") * width + jnp.arange(width, dtype=jnp.int32)
    tile_ids = jnp.sum((columns[None, :] >= tile_bounds[1:-1][:, None]).astype(jnp.int32), axis=0)
    one_hot = (tile_ids[None, :] == jnp.arange(tiles_count, dtype=jnp.int32)[:, None]).astype(
        jnp.float32
    )
    coefficients = jnp.einsum("tkl,tc->klc", filter_bands, one_hot, precision=lax.Precision.HIGHEST)
    filtered = vertical_filter(by_columns[0], coefficients).astype(jnp.bfloat16)
    moved_filtered = lax.all_to_all(filtered[None], "mem", split_axis=1, concat_axis=0, tiled=True)
    return jnp.sum(
        moved_pert.astype(jnp.float32) * moved_filtered.astype(jnp.float32)[None], axis=1
    )


def solution(mesh):
    in_specs = (P("mem", "geo", None, None), P(), P(), P(), P(), P(None, "mem", None, "geo"))
    out_specs = P(None, "mem", "geo")
    return jax.shard_map(body, mesh=mesh, in_specs=in_specs, out_specs=out_specs, check_vma=False)
```

profile of v0, /device:TPU:0, one launch (start us, length us, event | category | flops | bytes accessed | tf_op | source)
XLA Modules:
  0.0 219.2 jit_solution(1623861114880907975)
XLA Ops:
  0.0 1.1 copy.36
  1.1 1.9 fusion.36
  3.0 10.8 %select_add_fusion = f32[48,384]{1,0:T(8,128)S(1)} fusion(s32[48,384]{1,0:T(8,128)} %param.10, f32[]{:T(128)} %bitcast.16, f32[]{:T(128)} %bitcast.15, f32[]{:T(128)} %bitcast.14, f32[]{:T(128)} %bitcast.13, f32[]{:T(128)} %bitcast.12, f32[]{:T(128)} %bitcast.11, f32[]{:T(128)} %bitcast.10, f32[]{:T(128)} %bitcast.9, f32[]{:T(128)} %bitcast.8, f32[]{:T(128)} %bitcast.7, ...), kind=kLoop, calls=%fused_computation.47 | loop fusion | flops 866304 | bytes 147520 | tf_op jit(solution)/shard_map/add | solution.py:41
  14.1 10.9 %fusion.24 = (f32[48,384]{1,0:T(8,128)S(1)}, f32[48,384]{1,0:T(8,128)S(1)}, f32[48,384]{1,0:T(8,128)S(1)}, f32[48,384]{1,0:T(8,128)S(1)}) fusion(f32[48,383]{1,0:T(8,128)S(1)} %get-tuple-element.64, f32[48,1]{1,0:T(8,128)S(1)} %get-tuple-element.62, f32[48,1]{1,0:T(8,128)S(1)} %get-tuple-element.63, f32[48,383]{1,0:T(8,128)S(1)} %get-tuple-element.65, ...), kind=kLoop, calls=%fused_computation.44 | loop fusion | flops 1087488 | bytes 663616 | tf_op jit(solution)/shard_map/mul | solution.py:18
  24.9 10.2 %while.10 = (s32[]{:T(128)}, f32[1,8,48,384]{3,2,1,0:T(8,128)S(1)}, f32[48,384]{1,0:T(8,128)S(1)}, f32[48,384]{1,0:T(8,128)S(1)}, f32[48,384]{1,0:T(8,128)S(1)}, /*index=5*/f32[48,384]{1,0:T(8,128)S(1)}, s32[]{:T(128)}) while((s32[]{:T(128)}, f32[1,8,48,384]{3,2,1,0:T(8,128)S(1)}, f32[48,384]{1,0:T(8,128)S(1)}, f32[48,384]{1,0:T(8,128)S(1)}, ...), condition=%wide.region_1.2_spmd, body=%wide.region_0.1_spmd.sunk | while | flops 2359298 | bytes 8552525 | solution.py:43
  25.0 0.2 fusion.46
  25.4 0.6 fusion.47
  26.1 0.2 fusion.46
  26.4 0.6 fusion.47
  27.1 0.2 fusion.46
  27.4 0.6 fusion.47
  28.1 0.2 fusion.46
  28.5 0.6 fusion.47
  29.1 0.2 fusion.46
  29.5 0.6 fusion.47
  30.1 0.2 fusion.46
  30.5 0.6 fusion.47
  31.2 0.2 fusion.46
  31.5 0.6 fusion.47
  32.2 0.2 fusion.46
  32.5 0.6 fusion.47
  33.2 0.2 fusion.46
  33.6 0.6 fusion.47
  34.6 0.6 fusion.47
  35.2 5.5 %copy.21 = f32[1,8,48,384]{1,3,2,0:T(8,128)} copy(f32[1,8,48,384]{3,2,1,0:T(8,128)S(1)} %get-tuple-element.37) | data formatting | bytes 1179648 | tf_op jit(solution)/shard_map/while | solution.py:43
  40.7 0.5 broadcast.28
  41.2 83.6 %reduce.2 = f32[18432,8]{1,0:T(8,128)} reduce(f32[18432,1,8]{2,1,0:T(1,128)} %bitcast.70, f32[]{:T(128)} %broadcast.28), dimensions={1}, to_apply=%bitcast.62.reduce_sub_computation | reduce | bytes 1179652
  124.8 7.8 %reshape.43 = f32[4,1,36864]{2,1,0:T(1,128)} reshape(f32[18432,8]{1,0:T(8,128)} %reduce.2) | data formatting | bytes 1179648
  132.6 4.3 %all-to-all-start.1 = ((f32[4,1,36864]{2,1,0:T(1,128)}), f32[4,1,36864]{2,1,0:T(1,128)}, u32[]{:S(2)}, u32[]{:S(2)}) async-start(f32[4,1,36864]{2,1,0:T(1,128)} %reshape.43), calls=%async_computation.1 | async-start | bytes 1179648 | tf_op jit(solution)/shard_map/all_to_all | solution.py:45
  137.2 1.3 convolution_bitcast_fusion
  138.5 8.5 %all-to-all-done.1 = f32[4,1,36864]{2,1,0:T(1,128)} async-done(((f32[4,1,36864]{2,1,0:T(1,128)}), f32[4,1,36864]{2,1,0:T(1,128)}, u32[]{:S(2)}, u32[]{:S(2)}) %all-to-all-start.1) | async-done | bytes 589856 | tf_op jit(solution)/shard_map/all_to_all | solution.py:45
  147.0 3.3 %reduce.3 = f32[4,36864]{1,0:T(4,128)S(1)} reduce(f32[4,1,36864]{2,1,0:T(1,128)} %all-to-all-done.1, f32[]{:T(128)} %broadcast.28), dimensions={1}, to_apply=%all_to_all.11.reduce_sub_computation | reduce | bytes 1179652 | tf_op jit(solution)/shard_map/all_to_all | solution.py:45
  150.3 22.3 %reshape.44 = f32[18432,1,8]{2,1,0:T(1,128)} reshape(f32[4,36864]{1,0:T(4,128)S(1)} %reduce.3) | data formatting | bytes 1179648
  172.6 5.5 %copy.22 = f32[1,8,4,4608]{3,1,2,0:T(8,128)S(1)} copy(f32[1,8,4,4608]{1,3,2,0:T(8,128)} %bitcast.71) | data formatting | bytes 1179648 | tf_op jit(solution)/shard_map/all_to_all | solution.py:45
  178.1 0.4 fusion.20
  178.5 0.5 copy.27
  178.9 0.5 broadcast.30
  179.5 2.5 %reduce.4 = bf16[32,4608]{1,0:T(8,128)(2,1)S(1)} reduce(bf16[32,1,4608]{2,1,0:T(2,128)(2,1)S(1)} %bitcast.72, bf16[]{:T(256)} %broadcast.30), dimensions={1}, to_apply=%bitcast.69.reduce_sub_computation | reduce | bytes 589826
  181.9 0.9 reshape.45
  182.8 6.6 %all-to-all-start.2 = ((bf16[8,2,9216]{2,1,0:T(2,128)(2,1)}), bf16[8,2,9216]{2,1,0:T(2,128)(2,1)S(1)}, u32[]{:S(2)}, u32[]{:S(2)}) async-start(bf16[8,2,9216]{2,1,0:T(2,128)(2,1)} %reshape.45), calls=%async_computation.2 | async-start | bytes 589824 | tf_op jit(solution)/shard_map/all_to_all | solution.py:55
  189.4 1.4 copy.20
  190.8 7.9 %all-to-all-done.2 = bf16[8,2,9216]{2,1,0:T(2,128)(2,1)S(1)} async-done(((bf16[8,2,9216]{2,1,0:T(2,128)(2,1)}), bf16[8,2,9216]{2,1,0:T(2,128)(2,1)S(1)}, u32[]{:S(2)}, u32[]{:S(2)}) %all-to-all-start.2) | async-done | bytes 294944 | tf_op jit(solution)/shard_map/all_to_all | solution.py:55
  198.7 3.6 %all-to-all-start = ((bf16[2,1,32,4608]{3,0,1,2:T(2,128)(2,1)}), bf16[2,1,32,4608]{3,0,1,2:T(2,128)(2,1)S(1)}, u32[]{:S(2)}, u32[]{:S(2)}) async-start(bf16[2,1,32,4608]{3,0,1,2:T(2,128)(2,1)} %copy.20), calls=%async_computation | async-start | bytes 1179648 | tf_op jit(solution)/shard_map/all_to_all | solution.py:38
  202.3 0.2 reshape.46
  202.6 1.7 convert_reduce_fusion
  204.5 13.4 %all-to-all-done = bf16[2,1,32,4608]{3,0,1,2:T(2,128)(2,1)S(1)} async-done(((bf16[2,1,32,4608]{3,0,1,2:T(2,128)(2,1)}), bf16[2,1,32,4608]{3,0,1,2:T(2,128)(2,1)S(1)}, u32[]{:S(2)}, u32[]{:S(2)}) %all-to-all-start) | async-done | bytes 589856 | tf_op jit(solution)/shard_map/all_to_all | solution.py:38
  217.9 0.6 fusion.8
  218.5 0.7 copy.24
  (45 shorter events, 2.9 us)
Async XLA Ops:
  0.0 137.2 %copy-start = (f32[4,5,32]{2,0,1:T(4,128)S(1)}, f32[4,5,32]{2,0,1:T(4,128)}, u32[]{:S(2)}) copy-start(f32[4,5,32]{2,0,1:T(4,128)} %param.12) | copy-start | bytes 7684
  124.8 12.2 %copy-start.2 = (s32[5]{0:T(128)S(1)}, s32[5]{0:T(128)}, u32[]{:S(2)}) copy-start(s32[5]{0:T(128)} %param.11) | copy-start | bytes 64
  132.6 14.4 %all-to-all-start.1 = ((f32[4,1,36864]{2,1,0:T(1,128)}), f32[4,1,36864]{2,1,0:T(1,128)}, u32[]{:S(2)}, u32[]{:S(2)}) async-start(f32[4,1,36864]{2,1,0:T(1,128)} %reshape.43), calls=%async_computation.1 | async-start | bytes 1179648 | tf_op jit(solution)/shard_map/all_to_all | solution.py:45
  178.5 10.9 %copy-start.1 = (bf16[2,1,32,4608]{3,2,1,0:T(8,128)(2,1)S(1)}, bf16[2,1,32,4608]{3,2,1,0:T(8,128)(2,1)}, u32[]{:S(2)}) copy-start(bf16[2,1,32,4608]{3,2,1,0:T(8,128)(2,1)} %param.13) | copy-start | bytes 1769476
  182.8 15.8 %all-to-all-start.2 = ((bf16[8,2,9216]{2,1,0:T(2,128)(2,1)}), bf16[8,2,9216]{2,1,0:T(2,128)(2,1)S(1)}, u32[]{:S(2)}, u32[]{:S(2)}) async-start(bf16[8,2,9216]{2,1,0:T(2,128)(2,1)} %reshape.45), calls=%async_computation.2 | async-start | bytes 589824 | tf_op jit(solution)/shard_map/all_to_all | solution.py:55
  198.7 19.2 %all-to-all-start = ((bf16[2,1,32,4608]{3,0,1,2:T(2,128)(2,1)}), bf16[2,1,32,4608]{3,0,1,2:T(2,128)(2,1)S(1)}, u32[]{:S(2)}, u32[]{:S(2)}) async-start(bf16[2,1,32,4608]{3,0,1,2:T(2,128)(2,1)} %copy.20), calls=%async_computation | async-start | bytes 1179648 | tf_op jit(solution)/shard_map/all_to_all | solution.py:38
where the time goes:
time: 220 us; the launch traced here: 219 us
  other arithmetic  119 us (54%)
  local copies, waits for them, and re-layouts  53.6 us (24%)
  waiting for transfers between devices  29.8 us (14%)
  starting transfers between devices  14.5 us (7%)
    unnamed x2, other arithmetic  86 us
    unnamed x14, local copies, waits for them, and re-layouts  34.8 us
    all_to_all x1, waiting for transfers between devices, body(): lax.all_to_all(perturbation, 'mem', split_axis=2, concat_axis=1, tiled=True)  13.4 us
    mul x1, other arithmetic, face_weights(): 0.5 * (kappa_field + other)  10.9 us
    add x1, other arithmetic, body(): kappa_field + jnp.where(kappa_index == entry, kappa_table[entry], 0.0)  10.8 us
    all_to_all x1, waiting for transfers between devices, body(): lax.all_to_all(flattened, 'geo', split_axis=2, concat_axis=1, tiled=True)  8.52 us
    all_to_all x1, waiting for transfers between devices, body(): lax.all_to_all(filtered[None], 'mem', split_axis=1, concat_axis=0, tiled=...  7.85 us
    all_to_all x1, starting transfers between devices, body(): lax.all_to_all(filtered[None], 'mem', split_axis=1, concat_axis=0, tiled=...  6.57 us
  transfers between devices with their start and end apart: 3, of which 3 were waited for; matrix products, arithmetic and copies ran while one was open for 2% of the time, Pallas kernels for 0%

commit v1 on v0

--- a/solution.py
+++ b/solution.py
@@ -4,6 +4,18 @@
 from jax.sharding import PartitionSpec as P
 
 ITERS = 10
+
+
+def cut_along(x, dim, length):
+    shape = x.shape
+    blocks = x.reshape(*shape[:dim], length, shape[dim] // length, *shape[dim + 1 :])
+    return jnp.moveaxis(blocks, dim, 0)
+
+
+def laid_out(blocks, dim):
+    lengths = list(blocks.shape[1:])
+    lengths[dim] *= blocks.shape[0]
+    return jnp.moveaxis(blocks, 0, dim).reshape(lengths)
 
 
 def neighbours(state):
@@ -42,7 +54,15 @@
     weights = face_weights(kappa_field)
     state_field = lax.fori_loop(0, ITERS, lambda step, cur: diffuse_step(cur, weights), control)
     flattened = state_field.reshape(state_field.shape[0], state_field.shape[1], -1)
-    by_columns = lax.all_to_all(flattened, "geo", split_axis=2, concat_axis=1, tiled=True)
+    devices, index = (lax.axis_size("geo"), lax.axis_index("geo"))
+    parts = cut_along(flattened, 2, devices)
+    out = parts
+    for k in range(1, devices):
+        target, source = ((index + k) % devices, (index - k) % devices)
+        sent = lax.dynamic_index_in_dim(parts, target, 0)
+        theirs = lax.ppermute(sent, "geo", [(i, (i + k) % devices) for i in range(devices)])
+        out = lax.dynamic_update_slice_in_dim(out, theirs, source, axis=0)
+    by_columns = laid_out(out, 1)
     width = by_columns.shape[2]
     tiles_count = filter_bands.shape[0]
     columns = lax.axis_index("geo") * width + jnp.arange(width, dtype=jnp.int32)

time: 220 us -> 93.5 us (0.42)
  other arithmetic: 119 us -> 35.2 us
  local copies, waits for them, and re-layouts: 53.6 us -> 20.3 us
  waiting for transfers between devices: 29.8 us -> 21.5 us
    unnamed x2 -> x1, other arithmetic: 86 us -> 2.47 us
    unnamed x14, local copies, waits for them, and re-layouts: 34.8 us -> 6.18 us
    all_to_all x1 -> x0, waiting for transfers between devices: 8.52 us -> none  [body(): lax.all_to_all(flattened, 'geo', split_axis=2, concat_axis=1, tiled=True)]
    while x1 -> x0, local copies, waits for them, and re-layouts: 5.53 us -> none  [body(): lax.fori_loop(0, ITERS, lambda step, cur: diffuse_step(cur, weights), con...]
    all_to_all x1 -> x0, local copies, waits for them, and re-layouts: 5.48 us -> none  [body(): lax.all_to_all(flattened, 'geo', split_axis=2, concat_axis=1, tiled=True)]
    dynamic_update_slice x0 -> x3, local copies, waits for them, and re-layouts: none -> 4.73 us  [body(): out = lax.dynamic_update_slice_in_dim(out, theirs, source, axis=0)]
    ppermute x0 -> x3, starting transfers between devices: none -> 4.46 us  [body(): lax.ppermute(sent, 'geo', [(i, (i + k) % devices) for i in range(devices)])]
    all_to_all x1 -> x0, starting transfers between devices: 4.32 us -> none  [body(): lax.all_to_all(flattened, 'geo', split_axis=2, concat_axis=1, tiled=True)]
  transfers between devices with their start and end apart: 3 -> 5, of which waited for: 3 -> 2; matrix products, arithmetic and copies ran while one was open for 2% -> 11% of each run, Pallas kernels for 0% -> 0%
where the time goes in v1:
time: 93.5 us; the launch traced here: 92.7 us
  other arithmetic  35.2 us (38%)
  waiting for transfers between devices  21.5 us (23%)
  local copies, waits for them, and re-layouts  20.3 us (22%)
  starting transfers between devices  13.9 us (15%)
  matrix products  1.34 us (1%)
    all_to_all x1, waiting for transfers between devices, body(): lax.all_to_all(perturbation, 'mem', split_axis=2, concat_axis=1, tiled=True)  13.4 us
    mul x1, other arithmetic, face_weights(): 0.5 * (kappa_field + other)  11 us
    add x1, other arithmetic, body(): kappa_field + jnp.where(kappa_index == entry, kappa_table[entry], 0.0)  11 us
    all_to_all x1, waiting for transfers between devices, body(): lax.all_to_all(filtered[None], 'mem', split_axis=1, concat_axis=0, tiled=...  8.07 us
    unnamed x14, local copies, waits for them, and re-layouts  6.18 us
    all_to_all x1, starting transfers between devices, body(): lax.all_to_all(filtered[None], 'mem', split_axis=1, concat_axis=0, tiled=...  5.81 us
    add x10, other arithmetic, diffuse_step(): return state + update  5.51 us
    dynamic_update_slice x3, local copies, waits for them, and re-layouts, body(): out = lax.dynamic_update_slice_in_dim(out, theirs, source, axis=0)  4.73 us
  transfers between devices with their start and end apart: 5, of which 2 were waited for; matrix products, arithmetic and copies ran while one was open for 11% of the time, Pallas kernels for 0%

profile of v1, /device:TPU:0, one launch (start us, length us, event | category | flops | bytes accessed | tf_op | source)
XLA Modules:
  0.0 92.7 jit_solution(1264410682293870148)
XLA Ops:
  0.0 1.1 %copy.46 = f32[1,8,48,384]{3,2,1,0:T(8,128)S(1)} copy(f32[1,8,48,384]{3,2,1,0:T(8,128)} %param.8) | data formatting | bytes 1179648
  1.1 2.0 %fusion.36 = (f32[1]{0:T(128)}, f32[1]{0:T(128)}, f32[1]{0:T(128)}, f32[1]{0:T(128)}, f32[1]{0:T(128)}, /*index=5*/f32[1]{0:T(128)}, f32[1]{0:T(128)}, f32[1]{0:...) fusion(f32[16]{0:T(128)} %param.9), kind=kLoop, calls=%fused_computation.69 | loop fusion | bytes 128 | tf_op jit(solution)/shard_map/slice | solution.py:53
  3.0 11.0 %select_add_fusion = f32[48,384]{1,0:T(8,128)S(1)} fusion(s32[48,384]{1,0:T(8,128)} %param.10, f32[]{:T(128)} %bitcast.16, f32[]{:T(128)} %bitcast.15, f32[]{:T(128)} %bitcast.14, f32[]{:T(128)} %bitcast.13, f32[]{:T(128)} %bitcast.12, f32[]{:T(128)} %bitcast.11, f32[]{:T(128)} %bitcast.10, f32[]{:T(128)} %bitcast.9, f32[]{:T(128)} %bitcast.8, f32[]{:T(128)} %bitcast.7, ...), kind=kLoop, calls=%fused_computation.51 | loop fusion | flops 866304 | bytes 147520 | tf_op jit(solution)/shard_map/add | solution.py:53
  14.2 11.0 %fusion.24 = (f32[48,384]{1,0:T(8,128)S(1)}, f32[48,384]{1,0:T(8,128)S(1)}, f32[48,384]{1,0:T(8,128)S(1)}, f32[48,384]{1,0:T(8,128)S(1)}) fusion(f32[48,383]{1,0:T(8,128)S(1)} %get-tuple-element.67, f32[48,1]{1,0:T(8,128)S(1)} %get-tuple-element.65, f32[48,1]{1,0:T(8,128)S(1)} %get-tuple-element.66, f32[48,383]{1,0:T(8,128)S(1)} %get-tuple-element.68, ...), kind=kLoop, calls=%fused_computation.48 | loop fusion | flops 1087488 | bytes 663616 | tf_op jit(solution)/shard_map/mul | solution.py:30
  25.3 10.2 %while.10 = (s32[]{:T(128)}, f32[1,8,48,384]{3,2,1,0:T(8,128)S(1)}, f32[48,384]{1,0:T(8,128)S(1)}, f32[48,384]{1,0:T(8,128)S(1)}, f32[48,384]{1,0:T(8,128)S(1)}, /*index=5*/f32[48,384]{1,0:T(8,128)S(1)}, s32[]{:T(128)}) while((s32[]{:T(128)}, f32[1,8,48,384]{3,2,1,0:T(8,128)S(1)}, f32[48,384]{1,0:T(8,128)S(1)}, f32[48,384]{1,0:T(8,128)S(1)}, ...), condition=%wide.region_1.2_spmd, body=%wide.region_0.1_spmd.sunk | while | flops 2359298 | bytes 8552525 | solution.py:55
  25.4 0.2 fusion.46
  25.7 0.6 fusion.47
  26.7 0.6 fusion.47
  27.4 0.2 fusion.46
  27.8 0.6 fusion.47
  28.4 0.2 fusion.46
  28.8 0.6 fusion.47
  29.4 0.2 fusion.46
  29.8 0.6 fusion.47
  30.5 0.2 fusion.46
  30.8 0.6 fusion.47
  31.8 0.6 fusion.47
  32.5 0.2 fusion.46
  32.9 0.6 fusion.47
  33.5 0.2 fusion.46
  33.9 0.6 fusion.47
  34.9 0.6 fusion.47
  35.7 0.4 constant_dynamic-slice_fusion
  36.1 0.7 copy.34
  36.8 0.5 collective-permute-start
  37.3 0.7 copy.33
  37.9 2.5 %collective-permute-start.1 = (f32[1,1,8,4608]{3,2,0,1:T(8,128)}, f32[1,1,8,4608]{3,2,0,1:T(8,128)}, u32[]{:S(2)}, u32[]{:S(2)}) collective-permute-start(f32[1,1,8,4608]{3,2,0,1:T(8,128)} %bitcast.75), channel_id=1, source_target_pairs={{0,2},{1,3},{2,0},{3,1},{4,6},{5,7},{6,4},{7,5},{8,10},{9,11},{10,... | collective-permute-start | bytes 442376 | tf_op jit(solution)/shard_map/ppermute | solution.py:63
  40.5 0.7 copy.32
  41.1 1.5 %collective-permute-start.2 = (f32[1,1,8,4608]{3,2,0,1:T(8,128)}, f32[1,1,8,4608]{3,2,0,1:T(8,128)}, u32[]{:S(2)}, u32[]{:S(2)}) collective-permute-start(f32[1,1,8,4608]{3,2,0,1:T(8,128)} %bitcast.74), channel_id=1, source_target_pairs={{0,3},{1,0},{2,1},{3,2},{4,7},{5,4},{6,5},{7,6},{8,11},{9,8},{10,9... | collective-permute-start | bytes 442376 | tf_op jit(solution)/shard_map/ppermute | solution.py:63
  42.8 1.3 %convolution_bitcast_fusion = f32[5,32,4608]{2,1,0:T(8,128)S(1)} fusion(f32[4,5,32]{2,0,1:T(4,128)S(1)} %copy-done, s32[4608]{0:T(1024)S(1)} %convert_reduce_fusion.1), kind=kOutput, calls=%fused_computation.12 | convolution fusion | flops 35407872 | bytes 2970112 | tf_op jit(solution)/shard_map/tkl,tc->klc/dot_general | solution.py:73
  44.2 1.0 %copy.31 = f32[1,8,4,4608]{3,1,2,0:T(8,128)} copy(f32[1,8,4,4608]{3,2,1,0:T(4,128)S(1)} %reshape_reshape.3) | data formatting | bytes 1179648 | tf_op jit(solution)/shard_map/reshape;reshape | solution.py:11
  45.2 1.6 %constant_dynamic-update-slice_fusion.2 = f32[4,1,8,4608]{3,2,0,1:T(8,128)} fusion(f32[4,1,8,4608]{3,2,0,1:T(8,128)} %bitcast.80, f32[1,1,8,4608]{3,2,0,1:T(8,128)} %collective-permute-done, s32[]{:T(128)S(6)} %select_n.114), kind=kLoop, calls=%fused_computation.59 | loop fusion | bytes 294916 | tf_op jit(solution)/shard_map/dynamic_update_slice | solution.py:64
  46.7 1.6 %constant_dynamic-update-slice_fusion.1 = f32[4,1,8,4608]{3,2,0,1:T(8,128)} fusion(f32[4,1,8,4608]{3,2,0,1:T(8,128)} %constant_dynamic-update-slice_fusion.2, f32[1,1,8,4608]{3,2,0,1:T(8,128)} %collective-permute-done.1, s32[]{:T(128)S(6)} %select_n.118), kind=kLoop, calls=%fused_computation.57 | loop fusion | bytes 294916 | tf_op jit(solution)/shard_map/dynamic_update_slice | solution.py:64
  48.3 1.6 %constant_dynamic-update-slice_fusion = f32[4,1,8,4608]{3,2,0,1:T(8,128)} fusion(f32[4,1,8,4608]{3,2,0,1:T(8,128)} %constant_dynamic-update-slice_fusion.1, f32[1,1,8,4608]{3,2,0,1:T(8,128)} %collective-permute-done.2, s32[]{:T(128)S(6)} %select_n.122), kind=kLoop, calls=%fused_computation.55 | loop fusion | bytes 294916 | tf_op jit(solution)/shard_map/dynamic_update_slice | solution.py:64
  49.9 2.7 %fusion.20 = bf16[1,32,4608]{2,1,0:T(8,128)(2,1)S(1)} fusion(f32[32,4608]{1,0:T(8,128)} %bitcast.81, f32[5,32,4608]{2,1,0:T(8,128)S(1)} %convolution_bitcast_fusion), kind=kLoop, calls=%fused_computation.37 | loop fusion | flops 1622016 | bytes 3833856 | tf_op jit(solution)/shard_map/broadcast_in_dim | solution.py:75
  52.6 0.5 copy.35
  53.1 0.5 broadcast.34
  53.6 2.5 %reduce.2 = bf16[32,4608]{1,0:T(8,128)(2,1)S(1)} reduce(bf16[32,1,4608]{2,1,0:T(2,128)(2,1)S(1)} %bitcast.78, bf16[]{:T(256)} %broadcast.34), dimensions={1}, to_apply=%bitcast.77.reduce_sub_computation | reduce | bytes 589826
  56.0 0.9 reshape.41
  57.0 5.8 %all-to-all-start.1 = ((bf16[8,2,9216]{2,1,0:T(2,128)(2,1)}), bf16[8,2,9216]{2,1,0:T(2,128)(2,1)S(1)}, u32[]{:S(2)}, u32[]{:S(2)}) async-start(bf16[8,2,9216]{2,1,0:T(2,128)(2,1)} %reshape.41), calls=%async_computation.1 | async-start | bytes 589824 | tf_op jit(solution)/shard_map/all_to_all | solution.py:75
  62.8 1.4 %copy.18 = bf16[2,1,32,4608]{3,0,1,2:T(2,128)(2,1)} copy(bf16[2,1,32,4608]{3,2,1,0:T(8,128)(2,1)S(1)} %copy-done.1) | data formatting | bytes 1179648 | tf_op args[5]
  64.2 8.1 %all-to-all-done.1 = bf16[8,2,9216]{2,1,0:T(2,128)(2,1)S(1)} async-done(((bf16[8,2,9216]{2,1,0:T(2,128)(2,1)}), bf16[8,2,9216]{2,1,0:T(2,128)(2,1)S(1)}, u32[]{:S(2)}, u32[]{:S(2)}) %all-to-all-start.1) | async-done | bytes 294944 | tf_op jit(solution)/shard_map/all_to_all | solution.py:75
  72.3 3.6 %all-to-all-start = ((bf16[2,1,32,4608]{3,0,1,2:T(2,128)(2,1)}), bf16[2,1,32,4608]{3,0,1,2:T(2,128)(2,1)S(1)}, u32[]{:S(2)}, u32[]{:S(2)}) async-start(bf16[2,1,32,4608]{3,0,1,2:T(2,128)(2,1)} %copy.18), calls=%async_computation | async-start | bytes 1179648 | tf_op jit(solution)/shard_map/all_to_all | solution.py:50
  75.9 0.2 reshape.42
  76.1 1.7 %convert_reduce_fusion = f32[32,4608]{1,0:T(8,128)S(1)} fusion(bf16[32,1,4608]{2,1,0:T(2,128)(2,1)S(1)} %reshape.42), kind=kLoop, calls=%fused_computation.36 | loop fusion | flops 147456 | bytes 884736 | tf_op jit(solution)/shard_map/convert_element_type | solution.py:77
  78.0 13.4 %all-to-all-done = bf16[2,1,32,4608]{3,0,1,2:T(2,128)(2,1)S(1)} async-done(((bf16[2,1,32,4608]{3,0,1,2:T(2,128)(2,1)}), bf16[2,1,32,4608]{3,0,1,2:T(2,128)(2,1)S(1)}, u32[]{:S(2)}, u32[]{:S(2)}) %all-to-all-start) | async-done | bytes 589856 | tf_op jit(solution)/shard_map/all_to_all | solution.py:50
  91.4 0.6 fusion.8
  92.0 0.7 copy.21
  (51 shorter events, 3.5 us)
Async XLA Ops:
  0.0 42.8 %copy-start = (f32[4,5,32]{2,0,1:T(4,128)S(1)}, f32[4,5,32]{2,0,1:T(4,128)}, u32[]{:S(2)}) copy-start(f32[4,5,32]{2,0,1:T(4,128)} %param.12) | copy-start | bytes 7684
  35.5 7.1 %copy-start.2 = (s32[5]{0:T(128)S(1)}, s32[5]{0:T(128)}, u32[]{:S(2)}) copy-start(s32[5]{0:T(128)} %param.11) | copy-start | bytes 64
  36.8 8.4 %collective-permute-start = (f32[1,1,8,4608]{3,2,0,1:T(8,128)}, f32[1,1,8,4608]{3,2,0,1:T(8,128)}, u32[]{:S(2)}, u32[]{:S(2)}) collective-permute-start(f32[1,1,8,4608]{3,2,0,1:T(8,128)} %bitcast.76), channel_id=1, source_target_pairs={{0,1},{1,2},{2,3},{3,0},{4,5},{5,6},{6,7},{7,4},{8,9},{9,10},{10,1... | collective-permute-start | bytes 442376 | tf_op jit(solution)/shard_map/ppermute | solution.py:63
  37.9 8.8 %collective-permute-start.1 = (f32[1,1,8,4608]{3,2,0,1:T(8,128)}, f32[1,1,8,4608]{3,2,0,1:T(8,128)}, u32[]{:S(2)}, u32[]{:S(2)}) collective-permute-start(f32[1,1,8,4608]{3,2,0,1:T(8,128)} %bitcast.75), channel_id=1, source_target_pairs={{0,2},{1,3},{2,0},{3,1},{4,6},{5,7},{6,4},{7,5},{8,10},{9,11},{10,... | collective-permute-start | bytes 442376 | tf_op jit(solution)/shard_map/ppermute | solution.py:63
  41.1 7.2 %collective-permute-start.2 = (f32[1,1,8,4608]{3,2,0,1:T(8,128)}, f32[1,1,8,4608]{3,2,0,1:T(8,128)}, u32[]{:S(2)}, u32[]{:S(2)}) collective-permute-start(f32[1,1,8,4608]{3,2,0,1:T(8,128)} %bitcast.74), channel_id=1, source_target_pairs={{0,3},{1,0},{2,1},{3,2},{4,7},{5,4},{6,5},{7,6},{8,11},{9,8},{10,9... | collective-permute-start | bytes 442376 | tf_op jit(solution)/shard_map/ppermute | solution.py:63
  49.9 12.9 %copy-start.1 = (bf16[2,1,32,4608]{3,2,1,0:T(8,128)(2,1)S(1)}, bf16[2,1,32,4608]{3,2,1,0:T(8,128)(2,1)}, u32[]{:S(2)}) copy-start(bf16[2,1,32,4608]{3,2,1,0:T(8,128)(2,1)} %param.13) | copy-start | bytes 1769476
  57.0 15.3 %all-to-all-start.1 = ((bf16[8,2,9216]{2,1,0:T(2,128)(2,1)}), bf16[8,2,9216]{2,1,0:T(2,128)(2,1)S(1)}, u32[]{:S(2)}, u32[]{:S(2)}) async-start(bf16[8,2,9216]{2,1,0:T(2,128)(2,1)} %reshape.41), calls=%async_computation.1 | async-start | bytes 589824 | tf_op jit(solution)/shard_map/all_to_all | solution.py:75
  72.3 19.1 %all-to-all-start = ((bf16[2,1,32,4608]{3,0,1,2:T(2,128)(2,1)}), bf16[2,1,32,4608]{3,0,1,2:T(2,128)(2,1)S(1)}, u32[]{:S(2)}, u32[]{:S(2)}) async-start(bf16[2,1,32,4608]{3,0,1,2:T(2,128)(2,1)} %copy.18), calls=%async_computation | async-start | bytes 1179648 | tf_op jit(solution)/shard_map/all_to_all | solution.py:50
